TPU v7x, 256 devices: a 4x2x16 block of a 4x16x16 slice. The times are simulated.
256 devices in a mesh: groups: 2 (over y), context: 128 (over x, z, core).
Axes of the slice: x: 4, y: 2, z: 16, core: 2. Of those that a mesh axis runs over, the one named last changes fastest.
The devices are a block of a 4x16x16 slice.
Arguments:
- query_proj: bfloat16 [32768, 5120], P(('groups', 'context')), parts along dimension 0, may hold values from -100 to 100
- key_proj: bfloat16 [32768, 1024], P(('groups', 'context')), parts along dimension 0, may hold values from -100 to 100
- values: bfloat16 [32768, 1024], P(('groups', 'context')), parts along dimension 0, may hold values from -6 to 6
- grad_out: bfloat16 [32768, 5120], P(('groups', 'context')), parts along dimension 0, may hold values from -6 to 6
- query_gain: float32 [5120], replicated, may hold values from 0.1 to 1.9
- key_gain: float32 [1024], replicated, may hold values from 0.1 to 1.9
- segments: int32 [32768], P('groups'), parts along dimension 0, may hold values from 0 to 63, never falling along the last dimension, each value on 1 to 512 neighbouring positions
- layout: int32 [512], P('groups'), parts along dimension 0, may hold values from 0 to 255, as said below
Outputs:
- query_grad: bfloat16 [32768, 5120], P(('groups', 'context')), parts along dimension 0
- key_grad: bfloat16 [32768, 1024], P(('groups', 'context')), parts along dimension 0
- value_grad: bfloat16 [32768, 1024], P(('groups', 'context')), parts along dimension 0
- query_gain_grad: float32 [10240], P('groups'), parts along dimension 0
- key_gain_grad: float32 [2048], P('groups'), parts along dimension 0
There are 2 independent parts, one for each index of `groups`. A program takes and returns all parts, laid end to end along the dimension named above; an argument that names none is the same for every part. Nothing has to cross between parts.
Inputs may be any that keep to these rules, and one draw needn't show every extreme that they name: layout is a permutation of the spans; slots are ordered device by device, 2 to a device, and each aligned run of 8 slots holds the spans of one sequence of 512 positions in some order. `segments`: document numbers never fall along the stream; a document has 1 to 512 positions, and one has exactly 512.
All inputs are finite; a program needn't handle non-finite values.
Results may differ from a plain program's by a relative error of at most 0.0086.
Values may be sent and summed in bfloat16 or wider, within the bound.
No kernel may reach another device: no remote copies, remote signals or barrier semaphores. Data moves between devices by JAX's collectives and lax.ppermute only.
A program may use at most 128 MiB of HBM per device.

v0:
```python
import jax
import jax.numpy as jnp
from jax import lax
from jax.sharding import Mesh
from jax.sharding import PartitionSpec as P

QUERY_HEADS = 40
KEY_VALUE_HEADS = 8
HEAD_SIZE = 128
SPAN = 64
SEQ_BITS = 2
SEQ_DEVS = 4
LENGTH = 512
CONTEXT = ("context_0", "context_1", "context_2")
GROUPS_CONTEXT = ("groups", "context_0", "context_1", "context_2")


NORM_EPS = 1e-06
ROPE_BASE = 500000.0


def swapped(block, axis, apart):
    count = lax.axis_size(axis)
    route = []
    for low in range(count):
        high = low | 1 << apart
        if high != low and high < count:
            route += [(low, high), (high, low)]
    return lax.ppermute(block, axis, route)


def for_sending(array):

    def short(part):
        return part.astype(jnp.bfloat16) if part.dtype == jnp.float32 else part

    return jax.tree.map(short, array)


def by_axis(array, axes):
    for axis in axes:
        array = lax.psum(array, axis)
    return array


def rope_angles(positions, head_dim):
    half_dim = head_dim // 2
    inv_freq = jnp.power(ROPE_BASE, -2.0 * jnp.arange(half_dim, dtype=jnp.float32) / head_dim)
    angles = positions.astype(jnp.float32)[:, None] * inv_freq[None, :]
    return (jnp.cos(angles), jnp.sin(angles))


def rotate(inputs, cosine, sine, sign_flip):
    tok_rows = inputs.shape[0]
    half_dim = cosine.shape[1]
    halves = inputs.reshape(tok_rows, inputs.shape[1] // (2 * half_dim), 2, half_dim)
    lower_half = halves[:, :, 0]
    upper_half = halves[:, :, 1]
    cosine_b = cosine[:, None, :]
    sine_b = sine[:, None, :] * sign_flip
    rotated = jnp.stack(
        [lower_half * cosine_b - upper_half * sine_b, upper_half * cosine_b + lower_half * sine_b],
        axis=2,
    )
    return rotated.reshape(tok_rows, inputs.shape[1])


def norm_forward(inputs, gain_row):
    mean_sq = jnp.mean(inputs * inputs, axis=1, keepdims=True)
    factor = lax.rsqrt(mean_sq + NORM_EPS)
    return (inputs * factor * gain_row[None, :], factor)


def norm_backward(inputs, factor, gain_row, upstream):
    weighted = upstream * gain_row[None, :]
    inner_sum = jnp.mean(weighted * inputs, axis=1, keepdims=True)
    grad_in = factor * weighted - inputs * factor * factor * factor * inner_sum
    return (grad_in, jnp.sum(upstream * inputs * factor, axis=0))


def head_gradients(queries, key_rows, value_rows, grad_rows, allowed, query_head_group, head_dim):
    tok_rows = queries.shape[0]
    factor = head_dim ** (-0.5)
    query_heads = queries.reshape(tok_rows, query_head_group, head_dim)
    grad_heads = grad_rows.reshape(tok_rows, query_head_group, head_dim)
    scores = (
        jnp.einsum("qgd,kd->gqk", query_heads, key_rows, preferred_element_type=jnp.float32)
        * factor
    )
    scores = jnp.where(allowed[None], scores, -jnp.inf)
    row_max = jnp.max(scores, axis=2, keepdims=True)
    expo = jnp.exp(scores - row_max)
    attn_probs = expo / jnp.sum(expo, axis=2, keepdims=True)
    dprobs = jnp.einsum("qgd,kd->gqk", grad_heads, value_rows, preferred_element_type=jnp.float32)
    row_delta = jnp.sum(attn_probs * dprobs, axis=2, keepdims=True)
    dscores = (attn_probs * (dprobs - row_delta)).astype(jnp.bfloat16)
    probs_low = attn_probs.astype(jnp.bfloat16)
    query_part = (
        jnp.einsum("gqk,kd->qgd", dscores, key_rows, preferred_element_type=jnp.float32) * factor
    )
    key_part = (
        jnp.einsum("gqk,qgd->kd", dscores, query_heads, preferred_element_type=jnp.float32) * factor
    )
    value_part = jnp.einsum(
        "gqk,qgd->kd", probs_low, grad_heads, preferred_element_type=jnp.float32
    )
    return (query_part.reshape(tok_rows, query_head_group * head_dim), key_part, value_part)


def token_info(devices, tok_rows, layout, segments):
    local_index = jnp.arange(tok_rows, dtype=jnp.int32)
    slot_ids = devices[:, None] * (tok_rows // SPAN) + local_index[None, :] // SPAN
    positions = jnp.take(layout, slot_ids) * SPAN + local_index[None, :] % SPAN
    positions = positions.reshape(-1)
    return (positions, jnp.take(segments, positions))


def body(query_proj, key_proj, values, grad_out, query_gain, key_gain, segments, layout):
    tok_rows = query_proj.shape[0]
    my_index = lax.axis_index(CONTEXT)
    query_head_group = QUERY_HEADS // KEY_VALUE_HEADS
    group_width = query_head_group * HEAD_SIZE
    local_rank = my_index % SEQ_DEVS
    seq_base = my_index - local_rank
    positions, doc_query = token_info(jnp.reshape(my_index, (1,)), tok_rows, layout, segments)
    cosine, sine = rope_angles(positions % LENGTH, HEAD_SIZE)
    q_inputs = query_proj.astype(jnp.float32)
    k_inputs = key_proj.astype(jnp.float32)
    q_normed, q_factor = norm_forward(q_inputs, query_gain)
    k_normed, k_factor = norm_forward(k_inputs, key_gain)
    q_rope = rotate(q_normed, cosine, sine, 1.0).astype(jnp.bfloat16)
    k_rope = rotate(k_normed, cosine, sine, 1.0).astype(jnp.bfloat16)
    bit_order = list(range(SEQ_BITS))
    held_k, held_v = (k_rope, values)
    owners = jnp.reshape(local_rank, (1,))
    for bit in bit_order:
        got_k, got_v = swapped((held_k, held_v), CONTEXT, bit)
        held_k = jnp.concatenate([held_k, got_k], axis=0)
        held_v = jnp.concatenate([held_v, got_v], axis=0)
        owners = jnp.concatenate([owners, jnp.bitwise_xor(owners, 1 << bit)])
    pos_key, doc_key = token_info(seq_base + owners, tok_rows, layout, segments)
    allowed = (doc_key[None, :] == doc_query[:, None]) & (pos_key[None, :] <= positions[:, None])
    query_parts, key_parts, value_parts = ([], [], [])
    for key_value_head in range(KEY_VALUE_HEADS):
        query_part, key_part, value_part = head_gradients(
            q_rope[:, key_value_head * group_width : (key_value_head + 1) * group_width],
            held_k[:, key_value_head * HEAD_SIZE : (key_value_head + 1) * HEAD_SIZE],
            held_v[:, key_value_head * HEAD_SIZE : (key_value_head + 1) * HEAD_SIZE],
            grad_out[:, key_value_head * group_width : (key_value_head + 1) * group_width],
            allowed,
            query_head_group,
            HEAD_SIZE,
        )
        query_parts.append(query_part)
        key_parts.append(key_part)
        value_parts.append(value_part)
    dq_rope = jnp.concatenate(query_parts, axis=1)
    dk_all = jnp.concatenate(key_parts, axis=1)
    dv_all = jnp.concatenate(value_parts, axis=1)
    dq_normed = rotate(dq_rope, cosine, sine, -1.0)
    query_grad, q_gain_part = norm_backward(q_inputs, q_factor, query_gain, dq_normed)
    for bit in reversed(bit_order):
        half_rows = dk_all.shape[0] // 2
        back_k, back_v = swapped(
            (for_sending(dk_all[half_rows:]), for_sending(dv_all[half_rows:])), CONTEXT, bit
        )
        dk_all = dk_all[:half_rows] + back_k
        dv_all = dv_all[:half_rows] + back_v
    dk_normed = rotate(dk_all, cosine, sine, -1.0)
    key_grad, k_gain_part = norm_backward(k_inputs, k_factor, key_gain, dk_normed)
    q_gain_total, k_gain_total = (by_axis(q_gain_part, CONTEXT), by_axis(k_gain_part, CONTEXT))
    return (
        query_grad.astype(jnp.bfloat16),
        key_grad.astype(jnp.bfloat16),
        dv_all.astype(jnp.bfloat16),
        q_gain_total,
        k_gain_total,
    )


def solution(mesh):
    split = Mesh(
        mesh.devices.reshape(mesh.shape["groups"], 4, 16, 2),
        ("groups", "context_0", "context_1", "context_2"),
    )
    placed = (
        P(GROUPS_CONTEXT, None),
        P(GROUPS_CONTEXT, None),
        P(GROUPS_CONTEXT, None),
        P(GROUPS_CONTEXT, None),
        P(),
        P(),
        P("groups"),
        P("groups"),
    )
    return jax.shard_map(
        body,
        mesh=split,
        in_specs=placed,
        out_specs=(
            P(GROUPS_CONTEXT, None),
            P(GROUPS_CONTEXT, None),
            P(GROUPS_CONTEXT, None),
            P("groups"),
            P("groups"),
        ),
        check_vma=False,
    )
```

profile of v0, /device:TPU:40, one launch (start us, length us, event | category | flops | bytes accessed | tf_op | source)
XLA Modules:
  0.0 236.9 jit_solution(13967253927241340696)
XLA Ops:
  1.4 3.5 %gather_fusion.1 = s32[512]{0:T(512)S(1)} fusion(s32[256]{0:T(256)S(1)} %copy-done.2, s32[1024]{0:T(1024)S(1)} %pad_clamp_fusion.2), kind=kCustom, calls=%fused_computation.1 | custom fusion | bytes 6144 | tf_op jit(solution)/shard_map/jit(_take)/gather | solution.py:113
  9.8 3.1 %gather_fusion.2 = s32[512]{0:T(512)S(1)} fusion(s32[16384]{0:T(1024)S(1)} %copy-done, s32[1024]{0:T(1024)S(1)} %get-tuple-element.89), kind=kCustom, calls=%fused_computation.2 | custom fusion | bytes 6144 | tf_op jit(solution)/shard_map/jit(_take)/gather | solution.py:115
  14.5 2.2 fusion.9
  22.1 2.8 %collective-permute-start.1 = (bf16[256,1024]{1,0:T(8,128)(2,1)}, bf16[256,1024]{1,0:T(8,128)(2,1)}, u32[]{:S(2)}, u32[]{:S(2)}) collective-permute-start(bf16[256,1024]{1,0:T(8,128)(2,1)} %pad_maximum_fusion.3), channel_id=1, source_target_pairs={{0,2},{2,0},{1,3},{3,1},{4,6},{6,4},{5,7},{7,5},{8,10},{10,8},{9,1... | collective-permute-start | bytes 1572872 | tf_op jit(solution)/shard_map/ppermute | solution.py:29
  42.2 6.6 %collective-permute-done.3 = bf16[256,1024]{1,0:T(8,128)(2,1)} collective-permute-done((bf16[256,1024]{1,0:T(8,128)(2,1)}, bf16[256,1024]{1,0:T(8,128)(2,1)}, u32[]{:S(2)}, u32[]{:S(2)}) %collective-permute-start.3) | collective-permute-done | bytes 524320 | tf_op jit(solution)/shard_map/ppermute | solution.py:29
  54.1 2.5 %fusion.57 = f32[512,1024]{0,1:T(8,128)} fusion(bf16[128,5,128]{0,2,1:T(8,128)(2,1)} %bitcast.579, f32[5,128]{1,0:T(8,128)S(1)} %get-tuple-element.56, bf16[128,5,128]{0,2,1:T(8,128)(2,1)S(1)} %bitcast.564, pred[128,512]{0,1:T(8,128)(4,1)S(1)} %copy-done.54, bf16[512,1024]{1,0:T(8,128)(2,1)S(1)} %pad_maximum_fusion.2), kind=kOutput, calls=%fused_computation.120 | convolution fusion | flops 169411712 | bytes 790528 | tf_op jit(solution)/shard_map/gqk,qgd->kd/dot_general | solution.py:104
  61.9 2.5 %fusion.134 = (f32[5,128]{1,0:T(8,128)S(1)}, f32[5,128,512]{1,2,0:T(8,128)}) fusion(bf16[128,5,128]{0,2,1:T(8,128)(2,1)} %bitcast.556, pred[128,512]{0,1:T(8,128)(4,1)S(1)} %copy-done.54, bf16[512,1024]{1,0:T(8,128)(2,1)S(1)} %pad_maximum_fusion.2), kind=kOutput, calls=%fused_computation.312 | convolution fusion | flops 85197312 | bytes 1673728 | tf_op jit(solution)/shard_map/sub | solution.py:92
  68.6 2.5 %fusion.135 = (f32[5,128]{1,0:T(8,128)S(1)}, f32[5,128,512]{1,2,0:T(8,128)}) fusion(bf16[128,5,128]{0,2,1:T(8,128)(2,1)} %bitcast.553, pred[128,512]{0,1:T(8,128)(4,1)S(1)} %copy-done.54, bf16[512,1024]{1,0:T(8,128)(2,1)S(1)} %pad_maximum_fusion.2), kind=kOutput, calls=%fused_computation.313 | convolution fusion | flops 85197312 | bytes 1673728 | tf_op jit(solution)/shard_map/sub | solution.py:92
  71.1 1.9 multiply_reduce_fusion.4
  75.3 2.5 %fusion.136 = (f32[5,128]{1,0:T(8,128)S(1)}, f32[5,128,512]{1,2,0:T(8,128)}) fusion(bf16[128,5,128]{0,2,1:T(8,128)(2,1)} %bitcast.550, pred[128,512]{0,1:T(8,128)(4,1)S(1)} %copy-done.54, bf16[512,1024]{1,0:T(8,128)(2,1)S(1)} %pad_maximum_fusion.2), kind=kOutput, calls=%fused_computation.314 | convolution fusion | flops 85197312 | bytes 1673728 | tf_op jit(solution)/shard_map/sub | solution.py:92
  77.8 1.9 multiply_reduce_fusion.3
  82.0 2.5 %fusion.137 = (f32[5,128]{1,0:T(8,128)S(1)}, f32[5,128,512]{1,2,0:T(8,128)}) fusion(bf16[128,5,128]{0,2,1:T(8,128)(2,1)} %bitcast.547, pred[128,512]{0,1:T(8,128)(4,1)S(1)} %copy-done.54, bf16[512,1024]{1,0:T(8,128)(2,1)S(1)} %pad_maximum_fusion.2), kind=kOutput, calls=%fused_computation.315 | convolution fusion | flops 85197312 | bytes 1673728 | tf_op jit(solution)/shard_map/sub | solution.py:92
  84.5 1.9 multiply_reduce_fusion.2
  88.7 2.5 %fusion.138 = (f32[5,128]{1,0:T(8,128)S(1)}, f32[5,128,512]{1,2,0:T(8,128)}) fusion(bf16[128,5,128]{0,2,1:T(8,128)(2,1)} %bitcast.544, pred[128,512]{0,1:T(8,128)(4,1)S(1)} %copy-done.54, bf16[512,1024]{1,0:T(8,128)(2,1)S(1)} %pad_maximum_fusion.2), kind=kOutput, calls=%fused_computation.316 | convolution fusion | flops 85197312 | bytes 1673728 | tf_op jit(solution)/shard_map/sub | solution.py:92
  95.5 2.5 %fusion.139 = (f32[5,128]{1,0:T(8,128)S(1)}, f32[5,128,512]{1,2,0:T(8,128)}) fusion(bf16[128,5,128]{0,2,1:T(8,128)(2,1)} %bitcast.541, pred[128,512]{0,1:T(8,128)(4,1)S(1)} %copy-done.54, bf16[512,1024]{1,0:T(8,128)(2,1)S(1)} %pad_maximum_fusion.2), kind=kOutput, calls=%fused_computation.317 | convolution fusion | flops 85197312 | bytes 1673728 | tf_op jit(solution)/shard_map/sub | solution.py:92
  98.0 1.9 multiply_reduce_fusion
  101.8 2.1 slice.375
  110.0 3.0 %fusion.17 = (f32[5120]{0:T(1024)S(1)}, f32[128]{0:T(128)S(1)}) fusion(bf16[128,5120]{0,1:T(8,128)(2,1)S(1)} %copy.70, f32[128,40,2,64]{0,3,2,1:T(8,128)S(1)} %pad_maximum_fusion, f32[128]{0:T(128)S(1)} %add_rsqrt_fusion.1, f32[5120]{0:T(1024)S(1)} %copy-done.44), kind=kLoop, calls=%fused_computation.25 | loop fusion | flops 4582272 | bytes 3974144 | tf_op jit(solution)/shard_map/reduce_sum | solution.py:78
  123.7 2.1 slice.374
  126.0 3.5 %fusion.13 = bf16[128,5120]{0,1:T(8,128)(2,1)S(1)} fusion(bf16[128,5120]{0,1:T(8,128)(2,1)S(1)} %copy.70, f32[128,40,2,64]{0,3,2,1:T(8,128)} %copy-done.3, f32[128]{0:T(128)S(1)} %broadcast_multiply_fusion.2, f32[5120]{0:T(1024)S(1)} %copy-done.44, f32[128]{0:T(128)S(1)} %add_rsqrt_fusion.1), kind=kLoop, calls=%fused_computation.21 | loop fusion | flops 5898240 | bytes 5264384 | tf_op jit(solution)/shard_map/convert_element_type | solution.py:173
  132.8 6.2 %collective-permute-done.6 = bf16[256,1024]{0,1:T(8,128)(2,1)S(1)} collective-permute-done((bf16[256,1024]{0,1:T(8,128)(2,1)}, bf16[256,1024]{0,1:T(8,128)(2,1)S(1)}, u32[]{:S(2)}, u32[]{:S(2)}) %collective-permute-start.6) | collective-permute-done | bytes 524320 | tf_op jit(solution)/shard_map/ppermute | solution.py:29
  142.8 17.5 %all-reduce.1 = (f32[5120]{0:T(1024)S(1)}, f32[1024]{0:T(1024)S(1)}) all-reduce(f32[5120]{0:T(1024)S(1)} %get-tuple-element.15, f32[1024]{0:T(1024)S(1)} %get-tuple-element.17), channel_id=1, replica_groups=mesh['groups'=2,'context_0'=4,'context_1'=16,'context_2'=2] {'context_0'}, use_global_device_ids=true, to_apply=%region_29.30 | all-reduce | flops 6144 | bytes 49152 | tf_op jit(solution)/shard_map/psum | solution.py:42
  160.3 72.6 %all-reduce = (f32[5120]{0:T(1024)S(1)}, f32[1024]{0:T(1024)S(1)}) all-reduce(f32[5120]{0:T(1024)S(1)} %get-tuple-element.21, f32[1024]{0:T(1024)S(1)} %get-tuple-element.22), channel_id=1, replica_groups=mesh['groups'=2,'context_0'=4,'context_1'=16,'context_2'=2] {'context_1'}, use_global_device_ids=true, to_apply=%region_30.31 | all-reduce | flops 6144 | bytes 49152 | tf_op jit(solution)/shard_map/psum | solution.py:42
  232.9 4.0 %all-reduce.2 = (f32[5120]{0:T(1024)}, f32[1024]{0:T(1024)}) all-reduce(f32[5120]{0:T(1024)S(1)} %get-tuple-element.19, f32[1024]{0:T(1024)S(1)} %get-tuple-element.20), channel_id=1, replica_groups=mesh['groups'=2,'context_0'=4,'context_1'=16,'context_2'=2] {'context_2'}, use_global_device_ids=true, to_apply=%region_31.32 | all-reduce | flops 6144 | bytes 49152 | tf_op jit(solution)/shard_map/psum | solution.py:42
  (237 shorter events, 81.3 us)
Async XLA Ops:
  0.6 5.7 %copy-start = (s32[16384]{0:T(1024)S(1)}, s32[16384]{0:T(1024)}, u32[]{:S(2)}) copy-start(s32[16384]{0:T(1024)} %param.14) | copy-start | bytes 196612
  1.4 6.1 %copy-start.43 = (bf16[128,1024]{1,0:T(8,128)(2,1)S(1)}, bf16[128,1024]{1,0:T(8,128)(2,1)}, u32[]{:S(2)}) copy-start(bf16[128,1024]{1,0:T(8,128)(2,1)} %param.9) | copy-start | bytes 786436
  4.9 3.8 %copy-start.55 = (f32[1024]{0:T(1024)S(1)}, f32[1024]{0:T(1024)}, u32[]{:S(2)}) copy-start(f32[1024]{0:T(1024)} %param.13) | copy-start | bytes 12292
  9.0 4.0 %copy-start.12 = (bf16[128,5120]{1,0:T(8,128)(2,1)S(1)}, bf16[128,5120]{1,0:T(8,128)(2,1)}, u32[]{:S(2)}) copy-start(bf16[128,5120]{1,0:T(8,128)(2,1)} %param.8) | copy-start | bytes 3932164
  9.1 11.2 %collective-permute-start = (bf16[128,1024]{1,0:T(8,128)(2,1)S(1)}, bf16[128,1024]{1,0:T(8,128)(2,1)}, u32[]{:S(2)}, u32[]{:S(2)}) collective-permute-start(bf16[128,1024]{1,0:T(8,128)(2,1)S(1)} %copy.74), channel_id=1, source_target_pairs={{0,1},{1,0},{2,3},{3,2},{4,5},{5,4},{6,7},{7,6},{8,9},{9,8},{10,11... | collective-permute-start | bytes 786440 | tf_op jit(solution)/shard_map/ppermute | solution.py:29
  9.6 20.5 %collective-permute-start.2 = (bf16[128,1024]{1,0:T(8,128)(2,1)S(1)}, bf16[128,1024]{1,0:T(8,128)(2,1)}, u32[]{:S(2)}, u32[]{:S(2)}) collective-permute-start(bf16[128,1024]{1,0:T(8,128)(2,1)S(1)} %copy-done.20), channel_id=1, source_target_pairs={{0,1},{1,0},{2,3},{3,2},{4,5},{5,4},{6,7},{7,6},{8,9},{9,8},{10,11... | collective-permute-start | bytes 786440 | tf_op jit(solution)/shard_map/ppermute | solution.py:29
  22.1 17.4 %collective-permute-start.1 = (bf16[256,1024]{1,0:T(8,128)(2,1)}, bf16[256,1024]{1,0:T(8,128)(2,1)}, u32[]{:S(2)}, u32[]{:S(2)}) collective-permute-start(bf16[256,1024]{1,0:T(8,128)(2,1)} %pad_maximum_fusion.3), channel_id=1, source_target_pairs={{0,2},{2,0},{1,3},{3,1},{4,6},{6,4},{5,7},{7,5},{8,10},{10,8},{9,1... | collective-permute-start | bytes 1572872 | tf_op jit(solution)/shard_map/ppermute | solution.py:29
  30.0 3.6 %copy-start.25 = (bf16[128,640]{1,0:T(8,128)(2,1)S(1)}, bf16[128,640]{1,0:T(8,128)(2,1)}, u32[]{:S(2)}) copy-start(bf16[128,640]{1,0:T(8,128)(2,1)} %get-tuple-element.45) | copy-start | bytes 491524
  30.0 4.4 %copy-start.24 = (bf16[128,640]{1,0:T(8,128)(2,1)S(1)}, bf16[128,640]{1,0:T(8,128)(2,1)}, u32[]{:S(2)}) copy-start(bf16[128,640]{1,0:T(8,128)(2,1)} %get-tuple-element.44) | copy-start | bytes 491524
  30.0 5.3 %copy-start.23 = (bf16[128,640]{1,0:T(8,128)(2,1)S(1)}, bf16[128,640]{1,0:T(8,128)(2,1)}, u32[]{:S(2)}) copy-start(bf16[128,640]{1,0:T(8,128)(2,1)} %get-tuple-element.43) | copy-start | bytes 491524
  30.0 6.1 %copy-start.22 = (bf16[128,640]{1,0:T(8,128)(2,1)S(1)}, bf16[128,640]{1,0:T(8,128)(2,1)}, u32[]{:S(2)}) copy-start(bf16[128,640]{1,0:T(8,128)(2,1)} %get-tuple-element.42) | copy-start | bytes 491524
  30.1 6.9 %copy-start.21 = (bf16[128,640]{1,0:T(8,128)(2,1)S(1)}, bf16[128,640]{1,0:T(8,128)(2,1)}, u32[]{:S(2)}) copy-start(bf16[128,640]{1,0:T(8,128)(2,1)} %get-tuple-element.41) | copy-start | bytes 491524
  31.9 16.9 %collective-permute-start.3 = (bf16[256,1024]{1,0:T(8,128)(2,1)}, bf16[256,1024]{1,0:T(8,128)(2,1)}, u32[]{:S(2)}, u32[]{:S(2)}) collective-permute-start(bf16[256,1024]{1,0:T(8,128)(2,1)} %pad_maximum_fusion.4), channel_id=1, source_target_pairs={{0,2},{2,0},{1,3},{3,1},{4,6},{6,4},{5,7},{7,5},{8,10},{10,8},{9,1... | collective-permute-start | bytes 1572872 | tf_op jit(solution)/shard_map/ppermute | solution.py:29
  40.7 10.0 %copy-start.53 = (bf16[128,640]{0,1:T(8,128)(2,1)S(1)}, bf16[128,640]{0,1:T(8,128)(2,1)}, u32[]{:S(2)}) copy-start(bf16[128,640]{0,1:T(8,128)(2,1)} %copy.190) | copy-start | bytes 491524
  101.8 4.0 %copy-start.14 = (f32[128,5,128]{2,0,1:T(8,128)S(1)}, f32[128,5,128]{2,0,1:T(8,128)}, u32[]{:S(2)}) copy-start(f32[128,5,128]{2,0,1:T(8,128)} %convolution_multiply_fusion.13) | copy-start | bytes 983044
  101.8 4.0 %copy-start.15 = (f32[128,5,128]{2,0,1:T(8,128)S(1)}, f32[128,5,128]{2,0,1:T(8,128)}, u32[]{:S(2)}) copy-start(f32[128,5,128]{2,0,1:T(8,128)} %convolution_multiply_fusion.12) | copy-start | bytes 983044
  104.0 27.0 %collective-permute-start.4 = (bf16[256,1024]{0,1:T(8,128)(2,1)}, bf16[256,1024]{0,1:T(8,128)(2,1)}, u32[]{:S(2)}, u32[]{:S(2)}) collective-permute-start(bf16[256,1024]{0,1:T(8,128)(2,1)} %slice.375), channel_id=1, source_target_pairs={{0,2},{2,0},{1,3},{3,1},{4,6},{6,4},{5,7},{7,5},{8,10},{10,8},{9,1... | collective-permute-start | bytes 1572872 | tf_op jit(solution)/shard_map/ppermute | solution.py:29
  110.0 3.0 %copy-start.40 = (bf16[128,640]{0,1:T(8,128)(2,1)S(1)}, bf16[128,640]{0,1:T(8,128)(2,1)}, u32[]{:S(2)}) copy-start(bf16[128,640]{0,1:T(8,128)(2,1)} %get-tuple-element.39) | copy-start | bytes 491524
  110.0 3.0 %copy-start.47 = (bf16[128,640]{0,1:T(8,128)(2,1)S(1)}, bf16[128,640]{0,1:T(8,128)(2,1)}, u32[]{:S(2)}) copy-start(bf16[128,640]{0,1:T(8,128)(2,1)} %copy.191) | copy-start | bytes 491524
  125.7 13.2 %collective-permute-start.6 = (bf16[256,1024]{0,1:T(8,128)(2,1)}, bf16[256,1024]{0,1:T(8,128)(2,1)S(1)}, u32[]{:S(2)}, u32[]{:S(2)}) collective-permute-start(bf16[256,1024]{0,1:T(8,128)(2,1)} %slice.374), channel_id=1, source_target_pairs={{0,2},{2,0},{1,3},{3,1},{4,6},{6,4},{5,7},{7,5},{8,10},{10,8},{9,1... | collective-permute-start | bytes 1572872 | tf_op jit(solution)/shard_map/ppermute | solution.py:29
  131.0 8.0 %copy-start.19 = (f32[512,1024]{0,1:T(8,128)S(1)}, f32[512,1024]{0,1:T(8,128)}, u32[]{:S(2)}) copy-start(f32[512,1024]{0,1:T(8,128)} %fusion.50) | copy-start | bytes 6291460
  132.6 6.7 %collective-permute-start.5 = (bf16[128,1024]{0,1:T(8,128)(2,1)S(1)}, bf16[128,1024]{0,1:T(8,128)(2,1)S(1)}, u32[]{:S(2)}, u32[]{:S(2)}) collective-permute-start(bf16[128,1024]{0,1:T(8,128)(2,1)S(1)} %slice.377), channel_id=1, source_target_pairs={{0,1},{1,0},{2,3},{3,2},{4,5},{5,4},{6,7},{7,6},{8,9},{9,8},{10,11... | collective-permute-start | bytes 786440 | tf_op jit(solution)/shard_map/ppermute | solution.py:29
  139.2 1.7 collective-permute-start.7
  140.8 96.1 %copy-start.1 = (s32[16384]{0:T(1024)S(1)}, s32[16384]{0:T(1024)}, u32[]{:S(2)}) copy-start(s32[16384]{0:T(1024)} %param.14) | copy-start | bytes 196612
  (40 other events, 60.5 us)
where the time goes:
time: 239 us; the launch traced here: 237 us
  blocking collectives  94.1 us (39%)
  matrix products  60.7 us (25%)
  local copies, waits for them, and re-layouts  39.4 us (16%)
  other arithmetic  22.1 us (9%)
  waiting for transfers between devices  13.7 us (6%)
  starting transfers between devices  5.41 us (2%)
    psum x3, blocking collectives, by_axis(): array = lax.psum(array, axis)  94.1 us
    unnamed x134, local copies, waits for them, and re-layouts  21.9 us
    sub x8, matrix products, head_gradients(): expo = jnp.exp(scores - row_max)  18.1 us
    dot_general x8, matrix products, head_gradients(): jnp.einsum('qgd,kd->gqk', grad_heads, value_rows, preferred_element_type=...  15 us
    ppermute x8, waiting for transfers between devices, swapped(): return lax.ppermute(block, axis, route)  13.7 us
    dot_general x8, matrix products, head_gradients(): jnp.einsum('gqk,qgd->kd', probs_low, grad_heads, preferred_element_type=j...  13 us
    dot_general x8, matrix products, head_gradients(): jnp.einsum('gqk,qgd->kd', dscores, query_heads, preferred_element_type=jn...  8.41 us
    dot_general x8, matrix products, head_gradients(): jnp.einsum('gqk,kd->qgd', dscores, key_rows, preferred_element_type=jnp.f...  6.18 us
  transfers between devices with their start and end apart: 8, of which 3 were waited for; matrix products, arithmetic and copies ran while one was open for 22% of the time, Pallas kernels for 0%

commit v1 on v0

v1 whole, which is shorter than its diff:
```python
import functools

import jax
import jax.numpy as jnp
from jax import lax
from jax.experimental import pallas as pl
from jax.experimental.pallas import tpu as pltpu
from jax.sharding import Mesh
from jax.sharding import PartitionSpec as P

HEADS = 40
KV = 8
REP = HEADS // KV
D = 128
HALF = D // 2
SPAN = 64
SPANS = 8
LENGTH = 512
TOK = 128
QW = HEADS * D
KW = KV * D
GW = REP * D
EPS = 1e-06
ROPE_BASE = 500000.0
SCALE = D ** (-0.5)
LOG2E = 1.4426950408889634
X, Z, C = "context_0", "context_1", "context_2"
CONTEXT = (X, Z, C)
GROUPS_CONTEXT = ("groups",) + CONTEXT
F32 = jnp.float32
BF16 = jnp.bfloat16
NT = (((1,), (1,)), ((), ()))


def partner(block, axis, bits):
    count = lax.axis_size(axis)
    return lax.ppermute(block, axis, [(i, i ^ bits) for i in range(count)])


def roll_half(x):
    return pltpu.roll(x, HALF, 1)


def query_kernel(q_ref, gain_ref, cos_ref, sin_ref, rope_ref, factor_ref):
    acc = jnp.zeros((TOK, D), F32)
    for h in range(HEADS):
        x = q_ref[:, h * D : (h + 1) * D].astype(F32)
        acc = acc + x * x
    factor = lax.rsqrt(jnp.sum(acc, axis=1, keepdims=True) * (1.0 / QW) + EPS)
    factor_ref[...] = jnp.broadcast_to(factor, (TOK, D))
    fb = factor_ref[...]
    cos = cos_ref[...]
    sin = sin_ref[...]
    for h in range(HEADS):
        cols = slice(h * D, (h + 1) * D)
        x = q_ref[:, cols].astype(F32) * fb * gain_ref[:, cols]
        rope_ref[:, cols] = (x * cos + roll_half(x) * sin).astype(BF16)


def key_kernel(k0, k1, k2, k3, gain_ref, cos_ref, sin_ref, rope_ref, trans_ref, hat_ref):
    for b, k_ref in enumerate((k0, k1, k2, k3)):
        rows = slice(b * TOK, (b + 1) * TOK)
        acc = jnp.zeros((TOK, D), F32)
        for h in range(KV):
            x = k_ref[:, h * D : (h + 1) * D].astype(F32)
            acc = acc + x * x
        factor = lax.rsqrt(jnp.sum(acc, axis=1, keepdims=True) * (1.0 / KW) + EPS)
        cos = cos_ref[rows, :]
        sin = sin_ref[rows, :]
        for h in range(KV):
            cols = slice(h * D, (h + 1) * D)
            hat = k_ref[:, cols].astype(F32) * factor
            hat_ref[rows, cols] = hat
            x = hat * gain_ref[:, cols]
            out = x * cos + roll_half(x) * sin
            rope_ref[rows, cols] = out.astype(BF16)
            trans_ref[cols, rows] = out.T.astype(BF16)


def attention_kernel(
    qr_ref,
    g_ref,
    q_ref,
    kr_ref,
    kt_ref,
    hat_ref,
    v0,
    v1,
    v2,
    v3,
    bias_ref,
    cos_ref,
    sin_ref,
    cost_ref,
    sint_ref,
    factor_ref,
    qgain_ref,
    own_ref,
    far_ref,
    send_near_ref,
    send_diag_ref,
    gain_ref,
    qgrad_ref,
    v_scr,
    p_scr,
    ds_scr,
    q5_scr,
    g5_scr,
    w_scr,
    qs_scr,
    inner_scr,
):
    h = pl.program_id(0)

    @pl.when(h == 0)
    def _():
        inner_scr[...] = jnp.zeros_like(inner_scr)

    for b, ref in enumerate((v0, v1, v2, v3)):
        v_scr[b * TOK : (b + 1) * TOK, :] = ref[...]
    for i in range(REP):
        q5_scr[i * TOK : (i + 1) * TOK, :] = qr_ref[:, i * D : (i + 1) * D]
        g5_scr[i * TOK : (i + 1) * TOK, :] = g_ref[:, i * D : (i + 1) * D]
    keys = kr_ref[...]
    vals = v_scr[...]
    for i in range(REP):
        rows = slice(i * TOK, (i + 1) * TOK)
        s = lax.dot_general(keys, q5_scr[rows, :], NT, preferred_element_type=F32)
        s = s + bias_ref[...]
        m = jnp.max(s, axis=0, keepdims=True)
        e = jnp.exp2((s - m) * (SCALE * LOG2E))
        p = e * (1.0 / jnp.sum(e, axis=0, keepdims=True))
        dp = lax.dot_general(vals, g5_scr[rows, :], NT, preferred_element_type=F32)
        delta = jnp.sum(p * dp, axis=0, keepdims=True)
        p_scr[:, rows] = p.astype(BF16)
        ds_scr[:, rows] = (p * (dp - delta)).astype(BF16)
    dv = jnp.dot(p_scr[...], g5_scr[...], preferred_element_type=F32)
    dk = jnp.dot(ds_scr[...], q5_scr[...], preferred_element_type=F32) * SCALE
    own_ref[0] = dk[0:TOK]
    own_ref[1] = dv[0:TOK]
    send_near_ref[0] = dk[TOK : 2 * TOK].astype(BF16)
    send_near_ref[1] = dv[TOK : 2 * TOK].astype(BF16)
    far_ref[0] = dk[2 * TOK : 3 * TOK]
    far_ref[1] = dv[2 * TOK : 3 * TOK]
    send_diag_ref[0] = dk[3 * TOK :].astype(BF16)
    send_diag_ref[1] = dv[3 * TOK :].astype(BF16)
    dkn = dk * cos_ref[...] - roll_half(dk) * sin_ref[...]
    gain_ref[0, REP : REP + 1, :] = jnp.sum(dkn * hat_ref[...], axis=0, keepdims=True)

    dqt = jnp.dot(kt_ref[...], ds_scr[...], preferred_element_type=F32)
    cost = cost_ref[...]
    sint = sint_ref[...]
    acc = inner_scr[...]
    factor = factor_ref[...]
    for i in range(REP):
        cols = slice(i * D, (i + 1) * D)
        da = dqt[0:HALF, cols]
        db = dqt[HALF:, cols]
        dqn = jnp.concatenate([da * cost + db * sint, db * cost - da * sint], axis=0).T
        q = q_ref[:, cols].astype(F32)
        gain_ref[0, i : i + 1, :] = jnp.sum(dqn * q * factor, axis=0, keepdims=True)
        w = dqn * qgain_ref[:, cols]
        acc = acc + w * q
        w_scr[h, :, cols] = w
        qs_scr[h, :, cols] = q_ref[:, cols]
    inner_scr[...] = acc
    gain_ref[0, REP + 1 :, :] = jnp.zeros((8 - REP - 1, D), F32)

    @pl.when(h == KV - 1)
    def _():
        inner = jnp.sum(inner_scr[...], axis=1, keepdims=True) * (1.0 / QW)
        coef = factor * factor * factor * inner
        for j in range(KV):
            for i in range(REP):
                cols = slice(i * D, (i + 1) * D)
                out = factor * w_scr[j, :, cols] - qs_scr[j, :, cols].astype(F32) * coef
                qgrad_ref[:, j * GW + i * D : j * GW + (i + 1) * D] = out.astype(BF16)


def finish_kernel(own_ref, near_ref, far_ref, k_ref, gain_ref, cos_ref, sin_ref, kgrad_ref, vgrad_ref):
    acc = jnp.zeros((TOK, D), F32)
    for h in range(KV):
        x = k_ref[:, h * D : (h + 1) * D].astype(F32)
        acc = acc + x * x
    factor = lax.rsqrt(jnp.sum(acc, axis=1, keepdims=True) * (1.0 / KW) + EPS)
    cos = cos_ref[...]
    sin = sin_ref[...]
    acc = jnp.zeros((TOK, D), F32)
    parts = []
    for h in range(KV):
        cols = slice(h * D, (h + 1) * D)
        dv = own_ref[1, :, cols] + near_ref[1, :, cols].astype(F32) + far_ref[1, :, cols].astype(F32)
        vgrad_ref[:, cols] = dv.astype(BF16)
        dk = own_ref[0, :, cols] + near_ref[0, :, cols].astype(F32) + far_ref[0, :, cols].astype(F32)
        w = (dk * cos - roll_half(dk) * sin) * gain_ref[:, cols]
        acc = acc + w * k_ref[:, cols].astype(F32)
        parts.append(w)
    inner = jnp.sum(acc, axis=1, keepdims=True) * (1.0 / KW)
    coef = factor * factor * factor * inner
    for h in range(KV):
        cols = slice(h * D, (h + 1) * D)
        out = factor * parts[h] - k_ref[:, cols].astype(F32) * coef
        kgrad_ref[:, cols] = out.astype(BF16)


def shape(dims, dtype=F32):
    return jax.ShapeDtypeStruct(dims, dtype)


def whole(count):
    return [pl.BlockSpec(memory_space=pltpu.VMEM)] * count


PARAMS = dict(vmem_limit_bytes=32 * 1024 * 1024)


def pick(table, index):
    chosen = index[:, None] == jnp.arange(table.shape[0], dtype=jnp.int32)[None, :]
    chosen = chosen.reshape(chosen.shape + (1,) * (table.ndim - 1))
    return jnp.sum(jnp.where(chosen, table[None], 0), axis=1)


def sum_gains(part):
    part = part + partner(part, C, 1)
    part = part + partner(part, X, 1) + partner(part, X, 2) + partner(part, X, 3)
    part = part + partner(part, Z, 1) + partner(part, Z, 2) + partner(part, Z, 3)
    return part + partner(part, Z, 4) + partner(part, Z, 8) + partner(part, Z, 12)


def body(query_proj, key_proj, values, grad_out, query_gain, key_gain, segments, layout):
    my_index = lax.axis_index(CONTEXT)
    rank = my_index % 4
    sequence = my_index // 4

    far_k = partner(key_proj, Z, 1)
    near_k = partner(key_proj, C, 1)
    far_v = partner(values, Z, 1)
    near_v = partner(values, C, 1)
    diag_k = partner(far_k, C, 1)
    diag_v = partner(far_v, C, 1)

    slots = lax.dynamic_slice(layout, (sequence * SPANS,), (SPANS,)) % SPANS
    segs = lax.dynamic_slice(segments, (sequence * LENGTH,), (LENGTH,)).reshape(SPANS, SPAN)
    j = jnp.arange(SPANS, dtype=jnp.int32)
    order = pick(slots, jnp.bitwise_xor(rank, j // 2) * 2 + j % 2)
    doc = pick(segs, order).reshape(LENGTH)
    pos = (order[:, None] * SPAN + jnp.arange(SPAN, dtype=jnp.int32)[None, :]).reshape(LENGTH)
    allowed = (doc[:, None] == doc[None, :TOK]) & (pos[:, None] <= pos[None, :TOK])
    bias = jnp.where(allowed, 0.0, -jnp.inf).astype(F32)

    lane = jnp.arange(D, dtype=jnp.int32)
    inv_freq = jnp.power(ROPE_BASE, -2.0 * (lane % HALF).astype(F32) / D)
    angles = pos.astype(F32)[:, None] * inv_freq[None, :]
    cos = jnp.cos(angles)
    sin = jnp.sin(angles) * jnp.where(lane < HALF, -1.0, 1.0)[None, :]
    cost = cos[:TOK, :HALF].T * SCALE
    sint = sin[:TOK, HALF:].T * SCALE
    qgain = query_gain.reshape(1, QW)
    kgain = key_gain.reshape(1, KW)

    q_rope, factor = pl.pallas_call(
        query_kernel,
        out_shape=(shape((TOK, QW), BF16), shape((TOK, D))),
        in_specs=whole(4),
        out_specs=tuple(whole(2)),
        compiler_params=pltpu.CompilerParams(**PARAMS),
        name="query_prep",
    )(query_proj, qgain, cos[:TOK], sin[:TOK])

    k_rope, k_trans, k_hat = pl.pallas_call(
        key_kernel,
        out_shape=(shape((LENGTH, KW), BF16), shape((KW, LENGTH), BF16), shape((LENGTH, KW))),
        in_specs=whole(7),
        out_specs=tuple(whole(3)),
        compiler_params=pltpu.CompilerParams(**PARAMS),
        name="key_prep",
    )(key_proj, near_k, far_k, diag_k, kgain, cos, sin)

    def cols(rows, width):
        return pl.BlockSpec((rows, width), lambda h: (0, h))

    def full(rows, width):
        return pl.BlockSpec((rows, width), lambda h: (0, 0))

    pair = pl.BlockSpec((2, TOK, D), lambda h: (0, 0, h))
    own, far, send_near, send_diag, gains, query_grad = pl.pallas_call(
        attention_kernel,
        grid=(KV,),
        out_shape=(
            shape((2, TOK, KW)),
            shape((2, TOK, KW)),
            shape((2, TOK, KW), BF16),
            shape((2, TOK, KW), BF16),
            shape((KV, 8, D)),
            shape((TOK, QW), BF16),
        ),
        in_specs=[
            cols(TOK, GW),
            cols(TOK, GW),
            cols(TOK, GW),
            cols(LENGTH, D),
            pl.BlockSpec((D, LENGTH), lambda h: (h, 0)),
            cols(LENGTH, D),
            cols(TOK, D),
            cols(TOK, D),
            cols(TOK, D),
            cols(TOK, D),
            full(LENGTH, TOK),
            full(LENGTH, D),
            full(LENGTH, D),
            full(HALF, TOK),
            full(HALF, TOK),
            full(TOK, D),
            cols(1, GW),
        ],
        out_specs=(
            pair,
            pair,
            pair,
            pair,
            pl.BlockSpec((1, 8, D), lambda h: (h, 0, 0)),
            full(TOK, QW),
        ),
        scratch_shapes=[
            pltpu.VMEM((LENGTH, D), BF16),
            pltpu.VMEM((LENGTH, GW), BF16),
            pltpu.VMEM((LENGTH, GW), BF16),
            pltpu.VMEM((GW, D), BF16),
            pltpu.VMEM((GW, D), BF16),
            pltpu.VMEM((KV, TOK, GW), F32),
            pltpu.VMEM((KV, TOK, GW), BF16),
            pltpu.VMEM((TOK, D), F32),
        ],
        compiler_params=pltpu.CompilerParams(**PARAMS),
        name="attention",
    )(
        q_rope,
        grad_out,
        query_proj,
        k_rope,
        k_trans,
        k_hat,
        values,
        near_v,
        far_v,
        diag_v,
        bias,
        cos,
        sin,
        cost,
        sint,
        factor,
        qgain,
    )

    back_diag = partner(send_diag, C, 1)
    send_far = (far + back_diag.astype(F32)).astype(BF16)
    back_far = partner(send_far, Z, 1)
    back_near = partner(send_near, C, 1)
    gains = sum_gains(gains)
    key_grad, value_grad = pl.pallas_call(
        finish_kernel,
        out_shape=(shape((TOK, KW), BF16), shape((TOK, KW), BF16)),
        in_specs=whole(7),
        out_specs=tuple(whole(2)),
        compiler_params=pltpu.CompilerParams(**PARAMS),
        name="key_finish",
    )(own, back_near, back_far, key_proj, kgain, cos[:TOK], sin[:TOK])
    return (
        query_grad,
        key_grad,
        value_grad,
        gains[:, :REP].reshape(QW),
        gains[:, REP].reshape(KW),
    )


def solution(mesh):
    split = Mesh(
        mesh.devices.reshape(mesh.shape["groups"], 4, 16, 2),
        ("groups",) + CONTEXT,
    )
    rows = P(GROUPS_CONTEXT, None)
    placed = (rows, rows, rows, rows, P(), P(), P("groups"), P("groups"))
    return jax.shard_map(
        body,
        mesh=split,
        in_specs=placed,
        out_specs=(rows, rows, rows, P("groups"), P("groups")),
        check_vma=False,
    )
```

time: 239 us -> 108 us (0.45)
  blocking collectives: 94.1 us -> 0 us
  matrix products: 60.7 us -> 0 us
  starting transfers between devices: 5.41 us -> 41.5 us
  local copies, waits for them, and re-layouts: 39.4 us -> 9.97 us
  Pallas kernels: 0 us -> 23.4 us
  other arithmetic: 22.1 us -> 4.58 us
  waiting for transfers between devices: 13.7 us -> 27.2 us
    psum x3 -> x0, blocking collectives: 94.1 us -> none  [by_axis(): array = lax.psum(array, axis)]
    dot_general x32 -> x0, matrix products: 42.6 us -> none  [the longest x8 15 us: head_gradients(): jnp.einsum('qgd,kd->gqk', grad_heads, value_rows, preferred_element_type=...]
    ppermute x8 -> x19, starting transfers between devices: 5.41 us -> 41.5 us  [partner(): return lax.ppermute(block, axis, [(i, i ^ bits) for i in range(count)])]
    pallas_call x0 -> x4, Pallas kernels: none -> 23.4 us  [the longest x1 18.2 us: body(): pl.pallas_call(attention_kernel, grid=(KV,), out_shape=(shape((2, TOK, KW...]
    sub x8 -> x0, matrix products: 18.1 us -> none  [head_gradients(): expo = jnp.exp(scores - row_max)]
    unnamed x134 -> x26, local copies, waits for them, and re-layouts: 21.9 us -> 4.03 us
    ppermute x8 -> x19, waiting for transfers between devices: 13.7 us -> 27.2 us  [partner(): return lax.ppermute(block, axis, [(i, i ^ bits) for i in range(count)])]
    gather x4 -> x0, local copies, waits for them, and re-layouts: 9.04 us -> none  [the longest x2 4.76 us: token_info(): positions = jnp.take(layout, slot_ids) * SPAN + local_index[None, :] % SPAN]
  transfers between devices with their start and end apart: 8 -> 19, of which waited for: 3 -> 6; matrix products, arithmetic and copies ran while one was open for 22% -> 10% of each run, Pallas kernels for 0% -> 4%
where the time goes in v1:
time: 108 us; the launch traced here: 107 us
  starting transfers between devices  41.5 us (38%)
  waiting for transfers between devices  27.2 us (25%)
  Pallas kernels  23.4 us (22%)
  local copies, waits for them, and re-layouts  9.97 us (9%)
  other arithmetic  4.58 us (4%)
    ppermute x19, starting transfers between devices, partner(): return lax.ppermute(block, axis, [(i, i ^ bits) for i in range(count)])  41.5 us
    ppermute x19, waiting for transfers between devices, partner(): return lax.ppermute(block, axis, [(i, i ^ bits) for i in range(count)])  27.2 us
    pallas_call x1, Pallas kernels, body(): pl.pallas_call(attention_kernel, grid=(KV,), out_shape=(shape((2, TOK, KW...  18.2 us
    unnamed x26, local copies, waits for them, and re-layouts  4.03 us
    pallas_call x1, Pallas kernels, body(): pl.pallas_call(key_kernel, out_shape=(shape((LENGTH, KW), BF16), shape((K...  2.81 us
  transfers between devices with their start and end apart: 19, of which 6 were waited for; matrix products, arithmetic and copies ran while one was open for 10% of the time, Pallas kernels for 4%

profile of v1, /device:TPU:40, one launch (start us, length us, event | category | flops | bytes accessed | tf_op | source)
XLA Modules:
  0.0 107.5 jit_solution(346318818410596873)
XLA Ops:
  0.8 2.9 %collective-permute-start.4 = (bf16[128,1024]{1,0:T(8,128)(2,1)}, bf16[128,1024]{1,0:T(8,128)(2,1)S(1)}, u32[]{:S(2)}, u32[]{:S(2)}) collective-permute-start(bf16[128,1024]{1,0:T(8,128)(2,1)} %v0.1), channel_id=1, source_target_pairs={{0,2},{2,0},{4,6},{6,4},{8,10},{10,8},{12,14},{14,12},{16,18},{18,... | collective-permute-start | bytes 786440 | tf_op jit(solution)/shard_map/ppermute | solution.py:37
  3.9 0.8 and_select_fusion.2
  5.0 1.0 fusion
  6.8 0.8 dynamic_slice.7
  8.3 2.8 %collective-permute-done.4.v2 = bf16[128,1024]{1,0:T(8,128)(2,1)S(1)} collective-permute-done((bf16[128,1024]{1,0:T(8,128)(2,1)}, bf16[128,1024]{1,0:T(8,128)(2,1)S(1)}, u32[]{:S(2)}, u32[]{:S(2)}) %collective-permute-start.4) | collective-permute-done | bytes 262176 | tf_op jit(solution)/shard_map/ppermute | solution.py:37
  11.1 5.3 %collective-permute-done.1.k2 = bf16[128,1024]{1,0:T(8,128)(2,1)S(1)} collective-permute-done((bf16[128,1024]{1,0:T(8,128)(2,1)}, bf16[128,1024]{1,0:T(8,128)(2,1)S(1)}, u32[]{:S(2)}, u32[]{:S(2)}) %collective-permute-start.1) | collective-permute-done | bytes 262176 | tf_op jit(solution)/shard_map/ppermute | solution.py:37
  17.2 1.5 %copy.18.sint_ref = f32[64,128]{1,0:T(8,128)} copy(f32[64,128]{0,1:T(8,128)} %fusion.1) | data formatting | bytes 65536 | tf_op jit(solution)/shard_map/mul | solution.py:257
  18.7 1.5 %copy.17.cost_ref = f32[64,128]{1,0:T(8,128)} copy(f32[64,128]{0,1:T(8,128)} %fusion.2) | data formatting | bytes 65536 | tf_op jit(solution)/shard_map/mul | solution.py:256
  21.0 1.1 %query_prep.1 = (bf16[128,5120]{1,0:T(8,128)(2,1)S(1)}, f32[128,128]{1,0:T(8,128)S(1)}) custom-call(bf16[128,5120]{1,0:T(8,128)(2,1)S(1)} %copy-done, f32[1,5120]{1,0:T(1,128)S(1)} %bitcast.8, f32[128,128]{1,0:T(8,128)S(1)} %slice.36.cos_ref, f32[128,128]{1,0:T(8,128)S(1)} %slice.37.sin_ref), custom_call_target="tpu_custom_call" | custom-call | tf_op jit(solution)/shard_map/query_prep/pallas_call | solution.py:261
  22.1 0.9 and_select_fusion.bias_ref
  23.7 2.8 %key_prep.1 = (bf16[512,1024]{1,0:T(8,128)(2,1)S(1)}, bf16[1024,512]{1,0:T(8,128)(2,1)S(1)}, f32[512,1024]{1,0:T(8,128)S(1)}) custom-call(bf16[128,1024]{1,0:T(8,128)(2,1)S(1)} %copy-done.2, bf16[128,1024]{1,0:T(8,128)(2,1)S(1)} %collective-permute-done.k1, bf16[128,1024]{1,0:T(8,128)(2,1)S(1)} %collective-permute-done.1.k2, ...), custom_call_target="tpu_custom_call" | custom-call | tf_op jit(solution)/shard_map/key_prep/pallas_call | solution.py:270
  27.3 0.9 copy-done.5
  28.2 0.9 copy-done.7
  29.2 18.2 %attention.1 = (f32[2,128,1024]{2,1,0:T(8,128)S(1)}, f32[2,128,1024]{2,1,0:T(8,128)S(1)}, bf16[2,128,1024]{2,1,0:T(8,128)(2,1)}, bf16[2,128,1024]{2,1,0:T(8,128)...) custom-call(bf16[128,5120]{1,0:T(8,128)(2,1)S(1)} %get-tuple-element.18.qr_ref, ...), custom_call_target="tpu_custom_call" | custom-call | tf_op jit(solution)/shard_map/attention/pallas_call | solution.py:286
  48.4 1.1 collective-permute-done.9
  49.5 3.1 %collective-permute-start.12 = (f32[8,8,128]{2,1,0:T(8,128)S(1)}, f32[8,8,128]{2,1,0:T(8,128)S(1)}, u32[]{:S(2)}, u32[]{:S(2)}) collective-permute-start(f32[8,8,128]{2,1,0:T(8,128)S(1)} %add.124), channel_id=1, source_target_pairs={{0,96},{32,64},{64,32},{96,0},{1,97},{33,65},{65,33},{97,1},{2,98}... | collective-permute-start | bytes 98312 | tf_op jit(solution)/shard_map/ppermute | solution.py:37
  53.8 2.0 %collective-permute-start.8 = (bf16[2,128,1024]{2,1,0:T(8,128)(2,1)S(1)}, bf16[2,128,1024]{2,1,0:T(8,128)(2,1)S(1)}, u32[]{:S(2)}, u32[]{:S(2)}) collective-permute-start(bf16[2,128,1024]{2,1,0:T(8,128)(2,1)S(1)} %add_convert_fusion), channel_id=1, source_target_pairs={{0,2},{2,0},{4,6},{6,4},{8,10},{10,8},{12,14},{14,12},{16,18},{18,... | collective-permute-start | bytes 1572872 | tf_op jit(solution)/shard_map/ppermute | solution.py:37
  55.8 2.3 %collective-permute-done.11 = f32[8,8,128]{2,1,0:T(8,128)S(1)} collective-permute-done((f32[8,8,128]{2,1,0:T(8,128)S(1)}, f32[8,8,128]{2,1,0:T(8,128)S(1)}, u32[]{:S(2)}, u32[]{:S(2)}) %collective-permute-start.11) | collective-permute-done | bytes 32800 | tf_op jit(solution)/shard_map/ppermute | solution.py:37
  58.1 6.3 %collective-permute-start.15 = (f32[8,8,128]{2,1,0:T(8,128)S(1)}, f32[8,8,128]{2,1,0:T(8,128)S(1)}, u32[]{:S(2)}, u32[]{:S(2)}) collective-permute-start(f32[8,8,128]{2,1,0:T(8,128)S(1)} %add_add_fusion.2), channel_id=1, source_target_pairs={{0,6},{2,4},{4,2},{6,0},{8,14},{10,12},{12,10},{14,8},{16,22},{18,... | collective-permute-start | bytes 98312 | tf_op jit(solution)/shard_map/ppermute | solution.py:37
  65.1 8.3 %collective-permute-done.15 = f32[8,8,128]{2,1,0:T(8,128)S(1)} collective-permute-done((f32[8,8,128]{2,1,0:T(8,128)S(1)}, f32[8,8,128]{2,1,0:T(8,128)S(1)}, u32[]{:S(2)}, u32[]{:S(2)}) %collective-permute-start.15) | collective-permute-done | bytes 32800 | tf_op jit(solution)/shard_map/ppermute | solution.py:37
  73.4 18.6 %collective-permute-start.18 = (f32[8,8,128]{2,1,0:T(8,128)S(1)}, f32[8,8,128]{2,1,0:T(8,128)S(1)}, u32[]{:S(2)}, u32[]{:S(2)}) collective-permute-start(f32[8,8,128]{2,1,0:T(8,128)S(1)} %add_add_fusion.1), channel_id=1, source_target_pairs={{0,24},{2,26},{4,28},{6,30},{8,16},{10,18},{12,20},{14,22},{16,8},... | collective-permute-start | bytes 98312 | tf_op jit(solution)/shard_map/ppermute | solution.py:37
  92.0 5.5 %collective-permute-start.16 = (f32[8,8,128]{2,1,0:T(8,128)S(1)}, f32[8,8,128]{2,1,0:T(8,128)S(1)}, u32[]{:S(2)}, u32[]{:S(2)}) collective-permute-start(f32[8,8,128]{2,1,0:T(8,128)S(1)} %add_add_fusion.1), channel_id=1, source_target_pairs={{0,8},{2,10},{4,12},{6,14},{8,0},{10,2},{12,4},{14,6},{16,24},{18,... | collective-permute-start | bytes 98312 | tf_op jit(solution)/shard_map/ppermute | solution.py:37
  97.5 7.5 %collective-permute-done.17 = f32[8,8,128]{2,1,0:T(8,128)S(1)} collective-permute-done((f32[8,8,128]{2,1,0:T(8,128)S(1)}, f32[8,8,128]{2,1,0:T(8,128)S(1)}, u32[]{:S(2)}, u32[]{:S(2)}) %collective-permute-start.17) | collective-permute-done | bytes 32800 | tf_op jit(solution)/shard_map/ppermute | solution.py:37
  106.2 1.2 %key_finish.1 = (bf16[128,1024]{1,0:T(8,128)(2,1)}, bf16[128,1024]{1,0:T(8,128)(2,1)}) custom-call(f32[2,128,1024]{2,1,0:T(8,128)S(1)} %get-tuple-element.24.own_ref, bf16[2,128,1024]{2,1,0:T(8,128)(2,1)S(1)} %collective-permute-done.6.near_ref, bf16[2,128,1024]{2,1,0:T(8,128)(2,1)S(1)} %collective-permute-done.8.far_ref, bf16[128,1024]{1,0:T(8,128)(2,1)S(1)} %copy-done.2, ...), custom_call_target="tpu_custom_call" | custom-call | tf_op jit(solution)/shard_map/key_finish/pallas_call | solution.py:361
  (75 shorter events, 9.3 us)
Async XLA Ops:
  0.6 19.7 %copy-start = (bf16[128,5120]{1,0:T(8,128)(2,1)S(1)}, bf16[128,5120]{1,0:T(8,128)(2,1)}, u32[]{:S(2)}) copy-start(bf16[128,5120]{1,0:T(8,128)(2,1)} %q_ref.3) | copy-start | bytes 3932164
  0.6 25.9 %collective-permute-start.3 = (bf16[128,1024]{1,0:T(8,128)(2,1)}, bf16[128,1024]{1,0:T(8,128)(2,1)S(1)}, u32[]{:S(2)}, u32[]{:S(2)}) collective-permute-start(bf16[128,1024]{1,0:T(8,128)(2,1)} %v0.1), channel_id=1, source_target_pairs={{0,1},{1,0},{2,3},{3,2},{4,5},{5,4},{6,7},{7,6},{8,9},{9,8},{10,11... | collective-permute-start | bytes 786440 | tf_op jit(solution)/shard_map/ppermute | solution.py:37
  0.8 10.3 %collective-permute-start.4 = (bf16[128,1024]{1,0:T(8,128)(2,1)}, bf16[128,1024]{1,0:T(8,128)(2,1)S(1)}, u32[]{:S(2)}, u32[]{:S(2)}) collective-permute-start(bf16[128,1024]{1,0:T(8,128)(2,1)} %v0.1), channel_id=1, source_target_pairs={{0,2},{2,0},{4,6},{6,4},{8,10},{10,8},{12,14},{14,12},{16,18},{18,... | collective-permute-start | bytes 786440 | tf_op jit(solution)/shard_map/ppermute | solution.py:37
  3.7 12.7 %collective-permute-start.1 = (bf16[128,1024]{1,0:T(8,128)(2,1)}, bf16[128,1024]{1,0:T(8,128)(2,1)S(1)}, u32[]{:S(2)}, u32[]{:S(2)}) collective-permute-start(bf16[128,1024]{1,0:T(8,128)(2,1)} %k_ref.1), channel_id=1, source_target_pairs={{0,2},{2,0},{4,6},{6,4},{8,10},{10,8},{12,14},{14,12},{16,18},{18,... | collective-permute-start | bytes 786440 | tf_op jit(solution)/shard_map/ppermute | solution.py:37
  3.8 19.1 %collective-permute-start = (bf16[128,1024]{1,0:T(8,128)(2,1)}, bf16[128,1024]{1,0:T(8,128)(2,1)S(1)}, u32[]{:S(2)}, u32[]{:S(2)}) collective-permute-start(bf16[128,1024]{1,0:T(8,128)(2,1)} %k_ref.1), channel_id=1, source_target_pairs={{0,1},{1,0},{2,3},{3,2},{4,5},{5,4},{6,7},{7,6},{8,9},{9,8},{10,11... | collective-permute-start | bytes 786440 | tf_op jit(solution)/shard_map/ppermute | solution.py:37
  6.0 17.0 %copy-start.2 = (bf16[128,1024]{1,0:T(8,128)(2,1)S(1)}, bf16[128,1024]{1,0:T(8,128)(2,1)}, u32[]{:S(2)}) copy-start(bf16[128,1024]{1,0:T(8,128)(2,1)} %k_ref.1) | copy-start | bytes 786436
  11.1 15.4 %copy-start.4 = (bf16[128,1024]{1,0:T(8,128)(2,1)}, bf16[128,1024]{1,0:T(8,128)(2,1)S(1)}, u32[]{:S(2)}) copy-start(bf16[128,1024]{1,0:T(8,128)(2,1)S(1)} %collective-permute-done.4.v2) | copy-start | bytes 786436
  11.1 15.5 %collective-permute-start.5 = (bf16[128,1024]{1,0:T(8,128)(2,1)S(1)}, bf16[128,1024]{1,0:T(8,128)(2,1)S(1)}, u32[]{:S(2)}, u32[]{:S(2)}) collective-permute-start(bf16[128,1024]{1,0:T(8,128)(2,1)S(1)} %collective-permute-done.4.v2), channel_id=1, source_target_pairs={{0,1},{1,0},{2,3},{3,2},{4,5},{5,4},{6,7},{7,6},{8,9},{9,8},{10,11... | collective-permute-start | bytes 786440 | tf_op jit(solution)/shard_map/ppermute | solution.py:37
  16.3 6.6 %collective-permute-start.2 = (bf16[128,1024]{1,0:T(8,128)(2,1)S(1)}, bf16[128,1024]{1,0:T(8,128)(2,1)}, u32[]{:S(2)}, u32[]{:S(2)}) collective-permute-start(bf16[128,1024]{1,0:T(8,128)(2,1)S(1)} %collective-permute-done.1.k2), channel_id=1, source_target_pairs={{0,1},{1,0},{2,3},{3,2},{4,5},{5,4},{6,7},{7,6},{8,9},{9,8},{10,11... | collective-permute-start | bytes 786440 | tf_op jit(solution)/shard_map/ppermute | solution.py:37
  21.0 6.2 %copy-start.9 = (f32[64,128]{1,0:T(8,128)S(1)}, f32[64,128]{1,0:T(8,128)}, u32[]{:S(2)}) copy-start(f32[64,128]{1,0:T(8,128)} %copy.17.cost_ref) | copy-start | bytes 98308
  47.4 6.2 %collective-permute-start.7 = (bf16[2,128,1024]{2,1,0:T(8,128)(2,1)S(1)}, bf16[2,128,1024]{2,1,0:T(8,128)(2,1)S(1)}, u32[]{:S(2)}, u32[]{:S(2)}) collective-permute-start(bf16[2,128,1024]{2,1,0:T(8,128)(2,1)S(1)} %get-tuple-element.27), channel_id=1, source_target_pairs={{0,1},{1,0},{2,3},{3,2},{4,5},{5,4},{6,7},{7,6},{8,9},{9,8},{10,11... | collective-permute-start | bytes 1572872 | tf_op jit(solution)/shard_map/ppermute | solution.py:37
  47.9 1.6 %collective-permute-start.9 = (f32[8,8,128]{2,1,0:T(8,128)S(1)}, f32[8,8,128]{2,1,0:T(8,128)S(1)}, u32[]{:S(2)}, u32[]{:S(2)}) collective-permute-start(f32[8,8,128]{2,1,0:T(8,128)S(1)} %get-tuple-element.30), channel_id=1, source_target_pairs={{0,1},{1,0},{2,3},{3,2},{4,5},{5,4},{6,7},{7,6},{8,9},{9,8},{10,11... | collective-permute-start | bytes 98312 | tf_op jit(solution)/shard_map/ppermute | solution.py:37
  47.9 58.3 %collective-permute-start.6 = (bf16[2,128,1024]{2,1,0:T(8,128)(2,1)}, bf16[2,128,1024]{2,1,0:T(8,128)(2,1)S(1)}, u32[]{:S(2)}, u32[]{:S(2)}) collective-permute-start(bf16[2,128,1024]{2,1,0:T(8,128)(2,1)} %get-tuple-element.25), channel_id=1, source_target_pairs={{0,1},{1,0},{2,3},{3,2},{4,5},{5,4},{6,7},{7,6},{8,9},{9,8},{10,11... | collective-permute-start | bytes 1572872 | tf_op jit(solution)/shard_map/ppermute | solution.py:37
  49.5 6.3 %collective-permute-start.12 = (f32[8,8,128]{2,1,0:T(8,128)S(1)}, f32[8,8,128]{2,1,0:T(8,128)S(1)}, u32[]{:S(2)}, u32[]{:S(2)}) collective-permute-start(f32[8,8,128]{2,1,0:T(8,128)S(1)} %add.124), channel_id=1, source_target_pairs={{0,96},{32,64},{64,32},{96,0},{1,97},{33,65},{65,33},{97,1},{2,98}... | collective-permute-start | bytes 98312 | tf_op jit(solution)/shard_map/ppermute | solution.py:37
  52.6 5.4 %collective-permute-start.11 = (f32[8,8,128]{2,1,0:T(8,128)S(1)}, f32[8,8,128]{2,1,0:T(8,128)S(1)}, u32[]{:S(2)}, u32[]{:S(2)}) collective-permute-start(f32[8,8,128]{2,1,0:T(8,128)S(1)} %add.124), channel_id=1, source_target_pairs={{0,64},{32,96},{64,0},{96,32},{1,65},{33,97},{65,1},{97,33},{2,66}... | collective-permute-start | bytes 98312 | tf_op jit(solution)/shard_map/ppermute | solution.py:37
  53.2 4.9 %collective-permute-start.10 = (f32[8,8,128]{2,1,0:T(8,128)S(1)}, f32[8,8,128]{2,1,0:T(8,128)S(1)}, u32[]{:S(2)}, u32[]{:S(2)}) collective-permute-start(f32[8,8,128]{2,1,0:T(8,128)S(1)} %add.124), channel_id=1, source_target_pairs={{0,32},{32,0},{64,96},{96,64},{1,33},{33,1},{65,97},{97,65},{2,34}... | collective-permute-start | bytes 98312 | tf_op jit(solution)/shard_map/ppermute | solution.py:37
  53.6 52.6 %copy-start.12 = (f32[1024]{0:T(1024)S(1)}, f32[1024]{0:T(1024)}, u32[]{:S(2)}) copy-start(f32[1024]{0:T(1024)} %param.13) | copy-start | bytes 12292
  53.8 52.4 %collective-permute-start.8 = (bf16[2,128,1024]{2,1,0:T(8,128)(2,1)S(1)}, bf16[2,128,1024]{2,1,0:T(8,128)(2,1)S(1)}, u32[]{:S(2)}, u32[]{:S(2)}) collective-permute-start(bf16[2,128,1024]{2,1,0:T(8,128)(2,1)S(1)} %add_convert_fusion), channel_id=1, source_target_pairs={{0,2},{2,0},{4,6},{6,4},{8,10},{10,8},{12,14},{14,12},{16,18},{18,... | collective-permute-start | bytes 1572872 | tf_op jit(solution)/shard_map/ppermute | solution.py:37
  58.1 15.3 %collective-permute-start.15 = (f32[8,8,128]{2,1,0:T(8,128)S(1)}, f32[8,8,128]{2,1,0:T(8,128)S(1)}, u32[]{:S(2)}, u32[]{:S(2)}) collective-permute-start(f32[8,8,128]{2,1,0:T(8,128)S(1)} %add_add_fusion.2), channel_id=1, source_target_pairs={{0,6},{2,4},{4,2},{6,0},{8,14},{10,12},{12,10},{14,8},{16,22},{18,... | collective-permute-start | bytes 98312 | tf_op jit(solution)/shard_map/ppermute | solution.py:37
  64.4 9.1 %collective-permute-start.14 = (f32[8,8,128]{2,1,0:T(8,128)S(1)}, f32[8,8,128]{2,1,0:T(8,128)S(1)}, u32[]{:S(2)}, u32[]{:S(2)}) collective-permute-start(f32[8,8,128]{2,1,0:T(8,128)S(1)} %add_add_fusion.2), channel_id=1, source_target_pairs={{0,4},{2,6},{4,0},{6,2},{8,12},{10,14},{12,8},{14,10},{16,20},{18,... | collective-permute-start | bytes 98312 | tf_op jit(solution)/shard_map/ppermute | solution.py:37
  64.4 9.1 %collective-permute-start.13 = (f32[8,8,128]{2,1,0:T(8,128)S(1)}, f32[8,8,128]{2,1,0:T(8,128)S(1)}, u32[]{:S(2)}, u32[]{:S(2)}) collective-permute-start(f32[8,8,128]{2,1,0:T(8,128)S(1)} %add_add_fusion.2), channel_id=1, source_target_pairs={{0,2},{2,0},{4,6},{6,4},{8,10},{10,8},{12,14},{14,12},{16,18},{18,... | collective-permute-start | bytes 98312 | tf_op jit(solution)/shard_map/ppermute | solution.py:37
  73.4 24.1 %collective-permute-start.18 = (f32[8,8,128]{2,1,0:T(8,128)S(1)}, f32[8,8,128]{2,1,0:T(8,128)S(1)}, u32[]{:S(2)}, u32[]{:S(2)}) collective-permute-start(f32[8,8,128]{2,1,0:T(8,128)S(1)} %add_add_fusion.1), channel_id=1, source_target_pairs={{0,24},{2,26},{4,28},{6,30},{8,16},{10,18},{12,20},{14,22},{16,8},... | collective-permute-start | bytes 98312 | tf_op jit(solution)/shard_map/ppermute | solution.py:37
  92.0 13.0 %collective-permute-start.17 = (f32[8,8,128]{2,1,0:T(8,128)S(1)}, f32[8,8,128]{2,1,0:T(8,128)S(1)}, u32[]{:S(2)}, u32[]{:S(2)}) collective-permute-start(f32[8,8,128]{2,1,0:T(8,128)S(1)} %add_add_fusion.1), channel_id=1, source_target_pairs={{0,16},{2,18},{4,20},{6,22},{8,24},{10,26},{12,28},{14,30},{16,0},... | collective-permute-start | bytes 98312 | tf_op jit(solution)/shard_map/ppermute | solution.py:37
  92.0 13.0 %collective-permute-start.16 = (f32[8,8,128]{2,1,0:T(8,128)S(1)}, f32[8,8,128]{2,1,0:T(8,128)S(1)}, u32[]{:S(2)}, u32[]{:S(2)}) collective-permute-start(f32[8,8,128]{2,1,0:T(8,128)S(1)} %add_add_fusion.1), channel_id=1, source_target_pairs={{0,8},{2,10},{4,12},{6,14},{8,0},{10,2},{12,4},{14,6},{16,24},{18,... | collective-permute-start | bytes 98312 | tf_op jit(solution)/shard_map/ppermute | solution.py:37
  (8 other events, 22.7 us)
